TPU v7x, 128 devices: a whole 4x4x4 slice. The times are simulated.
128 devices in a mesh: grp: 2 (over x_hi), row: 64 (over y, z, x_lo, core).
Axes of the slice: x: 4 (x_hi: 2, x_lo: 2; x = x_hi * 2 + x_lo), y: 4, z: 4, core: 2. Of those that a mesh axis runs over, the one named last changes fastest.
Arguments:
- saved_rows: float32 [32, 512, 128, 128], P(None, None, ('grp', 'row')), may hold values from -3 to 3
- table_order: int32 [32], replicated, may hold values from 0 to 31, each once
- owner_shard: int32 [32, 128, 128, 1], P(None, ('grp', 'row')), may hold values from 0 to 63; in each aligned block of 128 rows (0 to 127, 128 to 255, ..., all dimensions but the last counted through in order) at most 6 rows name the same one
- row_in_shard: int32 [32, 128, 128], P(None, ('grp', 'row')), may hold values from 0 to 1023
- bag_owner: int32 [32, 128, 128], P(None, ('grp', 'row')), may hold values from 0 to 15, never falling along the last dimension, each value on 1 to 32 neighbouring positions
Outputs:
- pooled: float32 [2048, 32, 128], P(('grp', 'row'))
Inputs may be any that keep to these rules, and one draw needn't show every extreme that they name: `owner_shard`: among the 128 ids of one table and one device, no shard number occurs more than 6 times, and 6 is reached in some of these blocks. `bag_owner`: never falls along the last dimension; every sample has 1 to 32 ids of each table. `table_order`: each table number once.
All inputs are finite; a program needn't handle non-finite values.
Results may differ from a plain program's by a relative error of at most 0.00007.
Values sent between devices are 32-bit elements; how exact they have to be, the bound alone decides.
No kernel may reach another device: no remote copies, remote signals or barrier semaphores. Data moves between devices by JAX's collectives and lax.ppermute only.
A program may use at most 128 MiB of HBM per device.

v0:
```python
import jax
import jax.numpy as jnp
from jax import lax
from jax.sharding import PartitionSpec as P

SAMP_DEV = 16


def fetch_rows(restored, wanted):
    per_group, row_count, columns = restored.shape
    present = wanted >= 0
    safe_rows = jnp.maximum(wanted, 0)
    table_base = (jnp.arange(per_group, dtype=jnp.int32) * row_count).reshape(
        (1,) * (wanted.ndim - 2) + (per_group, 1)
    )
    flat_index = (safe_rows + table_base).reshape(-1)
    fetched = jnp.take(restored.reshape(per_group * row_count, columns), flat_index, axis=0)
    fetched = fetched.reshape(wanted.shape + (columns,))
    return jnp.where(present[..., None], fetched, 0.0)


def body(saved_rows, table_order, owner_shard, row_in_shard, bag_owner):
    groups = lax.axis_size("grp")
    shards = lax.axis_size("row")
    devices = groups * shards
    table_count, saved_depth, _, columns = saved_rows.shape
    per_group = table_count // groups
    row_block = saved_depth // shards
    picker = (table_order[:, None] == jnp.arange(table_count, dtype=jnp.int32)[None, :]).astype(
        jnp.float32
    )
    ordered_rows = jnp.einsum(
        "cu,uqd->cqd",
        picker,
        saved_rows.reshape(table_count, saved_depth, columns),
        precision=lax.Precision.HIGHEST,
    )
    parcel = ordered_rows.reshape(groups, per_group, shards, row_block, columns)
    parcel = jnp.transpose(parcel, (0, 2, 1, 3, 4)).reshape(
        devices, per_group, row_block, 1, columns
    )
    placed = lax.all_to_all(parcel, ("grp", "row"), split_axis=0, concat_axis=3, tiled=True)
    restored = placed.reshape(per_group, row_block * devices, columns)
    ids_count = row_in_shard.shape[2]
    capacity = 3 * ids_count // shards
    target_shard = owner_shard[table_order][:, 0, :, 0]
    local_row = row_in_shard[table_order][:, 0, :]
    sample_of = bag_owner[table_order][:, 0, :]
    matches = (
        target_shard[:, :, None] == jnp.arange(shards, dtype=jnp.int32)[None, None, :]
    ).astype(jnp.int32)
    slot_rank = jnp.sum(jnp.cumsum(matches, axis=1) * matches, axis=2) - 1
    order_pos = jnp.arange(table_count, dtype=jnp.int32)[:, None]
    group_of = order_pos // per_group
    within = order_pos % per_group
    requests = jnp.full((groups, shards, per_group, capacity), -1, jnp.int32)
    requests = requests.at[group_of, target_shard, within, slot_rank].set(local_row)
    returned = lax.all_to_all(
        fetch_rows(
            restored,
            lax.all_to_all(
                requests.reshape(devices, per_group, capacity),
                ("grp", "row"),
                split_axis=0,
                concat_axis=0,
                tiled=True,
            ),
        ),
        ("grp", "row"),
        split_axis=0,
        concat_axis=0,
        tiled=True,
    )
    returned = returned.reshape(groups, shards, per_group, capacity, columns)
    slot_key = target_shard * capacity + slot_rank
    slot_hits = (
        slot_key[:, :, None] == jnp.arange(shards * capacity, dtype=jnp.int32)[None, None, :]
    ).astype(jnp.float32)
    member = (sample_of[:, None, :] == jnp.arange(SAMP_DEV, dtype=jnp.int32)[None, :, None]).astype(
        jnp.float32
    )
    weights = jnp.einsum("csp,cpj->csj", member, slot_hits, precision=lax.Precision.HIGHEST)
    weights = weights.reshape(groups, per_group, SAMP_DEV, shards, capacity)
    pooled = jnp.einsum("gwsrk,grwkd->sgwd", weights, returned, precision=lax.Precision.HIGHEST)
    return pooled.reshape(SAMP_DEV, table_count, columns)


def solution(mesh):
    return jax.shard_map(
        body,
        mesh=mesh,
        in_specs=(
            P(None, None, ("grp", "row"), None),
            P(),
            P(None, ("grp", "row"), None, None),
            P(None, ("grp", "row"), None),
            P(None, ("grp", "row"), None),
        ),
        out_specs=P(("grp", "row"), None, None),
        check_vma=False,
    )
```

profile of v0, /device:TPU:1, one launch (start us, length us, event | category | flops | bytes accessed | tf_op | source)
XLA Modules:
  0.0 343.4 jit_solution(10617359534294073028)
XLA Ops:
  1.4 3.3 select_reduce_fusion
  5.0 0.7 multiply_reduce_fusion
  6.4 1.3 gather_fusion.1
  7.7 15.5 %scatter_custom_fusion = s32[12288]{0:T(1024)S(1)} fusion(s32[4096]{0:T(1024)S(1)} %select_bitcast_fusion, s32[4096]{0:T(1024)S(1)} %bitcast.58, s32[]{:T(128)} %constant.57.clone.1), kind=kCustom, calls=%fused_computation.31 | custom fusion | bytes 49156
  23.4 1.0 copy.67
  24.4 11.5 %all-to-all-start = ((s32[128,16,6]{1,2,0:T(8,128)}), s32[128,16,6]{1,2,0:T(8,128)S(1)}, u32[]{:S(2)}, u32[]{:S(2)}) async-start(s32[128,16,6]{1,2,0:T(8,128)} %bitcast.8), calls=%async_computation | async-start | bytes 1048576 | tf_op jit(solution)/shard_map/all_to_all | solution.py:61
  35.9 0.7 eq.80
  36.6 15.6 %fusion = f32[2,16,64,8,128]{4,1,3,2,0:T(8,128)} fusion(f32[64,8,128,32]{2,1,0,3:T(8,128)} %bitcast.52, s32[2,16]{1,0:T(2,128)S(1)} %eq.80), kind=kOutput, calls=%fused_computation.5 | convolution fusion | flops 805307392 | bytes 16777344 | tf_op jit(solution)/shard_map/cu,uqd->cqd/dot_general | solution.py:32
  52.2 10.2 %all-to-all-start.1 = ((f32[128,16,8,1,128]{4,1,2,3,0:T(8,128)}), f32[128,16,8,1,128]{4,1,2,3,0:T(8,128)}, u32[]{:S(2)}, u32[]{:S(2)}) async-start(f32[128,16,8,1,128]{4,1,2,3,0:T(8,128)} %bitcast.51), calls=%async_computation.1 | async-start | bytes 16777216 | tf_op jit(solution)/shard_map/all_to_all | solution.py:42
  63.3 0.8 reshape.224
  65.3 104.7 %all-to-all-done.1 = f32[128,16,8,1,128]{4,1,2,3,0:T(8,128)} async-done(((f32[128,16,8,1,128]{4,1,2,3,0:T(8,128)}), f32[128,16,8,1,128]{4,1,2,3,0:T(8,128)}, u32[]{:S(2)}, u32[]{:S(2)}) %all-to-all-start.1) | async-done | bytes 8388640 | tf_op jit(solution)/shard_map/all_to_all | solution.py:42
  170.0 11.4 %copy.58 = f32[1,16,8,128,1,128]{5,3,2,1,4,0:T(8,128)} copy(f32[1,16,8,128,1,128]{5,1,2,3,4,0:T(8,128)} %bitcast.20) | data formatting | bytes 16777216 | tf_op jit(solution)/shard_map/all_to_all | solution.py:42
  181.5 44.4 %gather_fusion.2 = f32[12288,128]{1,0:T(8,128)} fusion(f32[16384,128]{1,0:T(8,128)} %bitcast.50, s32[12288]{0:T(1024)S(1)} %broadcast_clamp_fusion), kind=kCustom, calls=%fused_computation.2 | custom fusion | bytes 12632064 | tf_op jit(solution)/shard_map/jit(_take)/gather | solution.py:17
  225.9 8.4 %gather.18 = f32[128,16,6,128]{3,2,1,0:T(8,128)} reshape(f32[12288,128]{1,0:T(8,128)} %gather_fusion.2) | data formatting | bytes 12582912 | tf_op jit(solution)/shard_map/jit(_take)/gather | solution.py:17
  234.2 6.7 %select_select_fusion = f32[128,16,6,128]{3,2,1,0:T(8,128)S(1)} fusion(f32[128,16,6,128]{3,2,1,0:T(8,128)} %gather.18, pred[128,16,6]{2,1,0:T(8,128)(4,1)S(1)} %copy.55, pred[128,16,6]{2,1,0:T(8,128)(4,1)S(1)} %copy.53), kind=kLoop, calls=%fused_computation.8 | loop fusion | flops 3145728 | bytes 12607488 | tf_op jit(solution)/shard_map/jit(_where)/select_n | solution.py:19
  241.0 4.2 %copy.60 = f32[128,16,6,128]{3,1,2,0:T(8,128)} copy(f32[128,16,6,128]{3,2,1,0:T(8,128)S(1)} %select_select_fusion) | data formatting | bytes 12582912 | tf_op jit(solution)/shard_map/jit(_where)/select_n | solution.py:19
  245.1 7.1 %all-to-all-start.2 = ((f32[128,16,6,128]{3,1,2,0:T(8,128)}), f32[128,16,6,128]{3,1,2,0:T(8,128)}, u32[]{:S(2)}, u32[]{:S(2)}) async-start(f32[128,16,6,128]{3,1,2,0:T(8,128)} %copy.60), calls=%async_computation.2 | async-start | bytes 12582912 | tf_op jit(solution)/shard_map/all_to_all | solution.py:58
  252.8 2.1 fusion.5
  254.9 2.0 copy.61
  256.9 5.1 %reshape.226 = f32[2,16,16,64,6]{1,0,4,3,2:T(2,128)} reshape(f32[32,16,384]{0,2,1:T(8,128)S(1)} %copy.61) | data formatting | bytes 1572864 | tf_op jit(solution)/shard_map/reshape | solution.py:83
  262.0 7.9 %copy.63 = f32[2,16,16,64,6]{3,2,4,1,0:T(8,128)S(1)} copy(f32[2,16,16,64,6]{1,0,4,3,2:T(2,128)} %reshape.226) | data formatting | bytes 1572864 | tf_op jit(solution)/shard_map/reshape | solution.py:83
  269.9 61.4 %all-to-all-done.2 = f32[128,16,6,128]{3,1,2,0:T(8,128)} async-done(((f32[128,16,6,128]{3,1,2,0:T(8,128)}), f32[128,16,6,128]{3,1,2,0:T(8,128)}, u32[]{:S(2)}, u32[]{:S(2)}) %all-to-all-start.2) | async-done | bytes 6291488 | tf_op jit(solution)/shard_map/all_to_all | solution.py:58
  331.3 11.3 %fusion.3 = f32[2,16,128,16,1]{2,3,4,1,0:T(8,128)S(1)} fusion(f32[2,16,16,64,6]{3,2,4,1,0:T(8,128)S(1)} %copy.63, f32[2,64,16,6,128]{4,2,3,1,0:T(8,128)} %bitcast.23), kind=kOutput, calls=%fused_computation.9 | convolution fusion | flops 301989888 | bytes 7340032 | tf_op jit(solution)/shard_map/gwsrk,grwkd->sgwd/dot_general | solution.py:84
  342.6 0.8 copy.64
  (30 shorter events, 5.1 us)
Async XLA Ops:
  0.0 0.7 copy-start
  24.4 27.8 %all-to-all-start = ((s32[128,16,6]{1,2,0:T(8,128)}), s32[128,16,6]{1,2,0:T(8,128)S(1)}, u32[]{:S(2)}, u32[]{:S(2)}) async-start(s32[128,16,6]{1,2,0:T(8,128)} %bitcast.8), calls=%async_computation | async-start | bytes 1048576 | tf_op jit(solution)/shard_map/all_to_all | solution.py:61
  52.2 117.8 %all-to-all-start.1 = ((f32[128,16,8,1,128]{4,1,2,3,0:T(8,128)}), f32[128,16,8,1,128]{4,1,2,3,0:T(8,128)}, u32[]{:S(2)}, u32[]{:S(2)}) async-start(f32[128,16,8,1,128]{4,1,2,3,0:T(8,128)} %bitcast.51), calls=%async_computation.1 | async-start | bytes 16777216 | tf_op jit(solution)/shard_map/all_to_all | solution.py:42
  245.1 7.1 %copy-start.2 = (s32[32,1,128]{2,1,0:T(1,128)S(1)}, s32[32,1,128]{2,1,0:T(1,128)}, u32[]{:S(2)}) copy-start(s32[32,1,128]{2,1,0:T(1,128)} %param.9) | copy-start | bytes 49156
  245.1 86.2 %all-to-all-start.2 = ((f32[128,16,6,128]{3,1,2,0:T(8,128)}), f32[128,16,6,128]{3,1,2,0:T(8,128)}, u32[]{:S(2)}, u32[]{:S(2)}) async-start(f32[128,16,6,128]{3,1,2,0:T(8,128)} %copy.60), calls=%async_computation.2 | async-start | bytes 12582912 | tf_op jit(solution)/shard_map/all_to_all | solution.py:58
  262.0 81.3 %copy-start.1 = (s32[32,1,128,1]{2,3,1,0:T(1,128)S(1)}, s32[32,1,128,1]{2,3,1,0:T(1,128)}, u32[]{:S(2)}) copy-start(s32[32,1,128,1]{2,3,1,0:T(1,128)} %param.7) | copy-start | bytes 49156
where the time goes:
time: 345 us; the launch traced here: 343 us
  waiting for transfers between devices  166 us (48%)
  local copies, waits for them, and re-layouts  107 us (31%)
  matrix products  29 us (8%)
  starting transfers between devices  28.8 us (8%)
  other arithmetic  12.4 us (4%)
    all_to_all x1, waiting for transfers between devices, body(): lax.all_to_all(parcel, ('grp', 'row'), split_axis=0, concat_axis=3, tiled...  105 us
    all_to_all x1, waiting for transfers between devices, body(): lax.all_to_all(fetch_rows(restored, lax.all_to_all(requests.reshape(devic...  61.4 us
    gather x2, local copies, waits for them, and re-layouts, fetch_rows(): jnp.take(restored.reshape(per_group * row_count, columns), flat_index, ax...  52.8 us
    unnamed x8, local copies, waits for them, and re-layouts  15.7 us
    dot_general x1, matrix products, body(): jnp.einsum('cu,uqd->cqd', picker, saved_rows.reshape(table_count, saved_d...  15.6 us
    reshape x2, local copies, waits for them, and re-layouts, body(): weights = weights.reshape(groups, per_group, SAMP_DEV, shards, capacity)  12.9 us
    all_to_all x1, starting transfers between devices, body(): lax.all_to_all(requests.reshape(devices, per_group, capacity), ('grp', 'r...  11.5 us
    all_to_all x1, local copies, waits for them, and re-layouts, body(): lax.all_to_all(parcel, ('grp', 'row'), split_axis=0, concat_axis=3, tiled...  11.4 us
  transfers between devices with their start and end apart: 3, of which 2 were waited for; matrix products, arithmetic and copies ran while one was open for 11% of the time, Pallas kernels for 0%

commit v1 on v0

v1 whole, which is shorter than its diff:
```python
import jax
import jax.numpy as jnp
from jax import lax
from jax.experimental import pallas as pl
from jax.experimental.pallas import tpu as pltpu
from jax.sharding import Mesh, PartitionSpec as P

TABLES = 32
DEPTH = 512
WIDTH = 128
DEVICES = 128
IDS = 128
SAMP = 16
SPAN = 520
ZERO = 516


def place(k):
    return (k >> 6) * 2 + ((k >> 1) & 1), (k >> 4) & 3, (k >> 2) & 3, k & 1


def label(k):
    x, y, z, c = place(k)
    return (((x - z) & 3) * 4 + ((y - z) & 3)) * 2 + c


PLANES = [sorted((k for k in range(DEVICES) if place(k)[2] == z), key=label) for z in range(4)]
HOLDERS = [[PLANES[z][t] for z in range(4)] for t in range(TABLES)]
EVERYONE = [sum(PLANES, [])]


def lookup_kernel(addr, ends, table, out, *sums):
    blocks = len(sums)

    def step(i, carry):
        for j, prefix in enumerate(sums):
            ids = (i * blocks + j) * IDS
            total = jnp.zeros((1, WIDTH), jnp.float32)
            for p in range(IDS):
                total = total + table[pl.ds(addr[ids + p], 1), :]
                prefix[p + 1 : p + 2, :] = total
        for j, prefix in enumerate(sums):
            bag = (i * blocks + j) * SAMP
            below = jnp.zeros((1, WIDTH), jnp.float32)
            for b in range(SAMP):
                upto = prefix[pl.ds(ends[bag + b], 1), :]
                out[pl.ds(bag + b, 1), :] = upto - below
                below = upto
        return carry

    lax.fori_loop(0, DEVICES // blocks, step, 0)


def finish_kernel(order, parts, out):
    for c in range(TABLES):
        t = order[c]
        total = (parts[0, t] + parts[1, t]) + (parts[2, t] + parts[3, t])
        out[:, c, :] = total


def body(saved_rows, table_order, owner_shard, row_in_shard, bag_owner):
    me = lax.axis_index("d")
    x, y, z, c = place(me)
    ids = owner_shard[:, 0, :, 0] * 1024 + row_in_shard[:, 0, :]
    bags = bag_owner[:, 0, :]
    ends = jnp.sum(
        (bags[:, None, :] <= jnp.arange(IDS, dtype=jnp.int32)[None, :, None]).astype(jnp.int32), axis=2
    )
    notes = jnp.stack([ids, ends], axis=1).astype(jnp.float32)
    parcel = jnp.concatenate(
        [
            saved_rows.reshape(TABLES, DEPTH, WIDTH),
            jnp.pad(notes, ((0, 0), (0, SPAN - DEPTH - 2), (0, 0))),
        ],
        axis=1,
    )
    held = lax.all_to_all(parcel, "d", split_axis=0, concat_axis=0, tiled=True, axis_index_groups=PLANES)
    notes = held[:, DEPTH : DEPTH + 2]
    notes = lax.all_gather(notes, "d", axis_index_groups=HOLDERS, axis=0, tiled=True)
    notes = notes.astype(jnp.int32)
    wanted = notes[:, 0, :]
    source = wanted & 127
    addr = label(source) * SPAN + (wanted >> 7)
    addr = jnp.where(place(source)[2] == z, addr, ZERO)
    blocks = 4
    partial = pl.pallas_call(
        lookup_kernel,
        out_shape=jax.ShapeDtypeStruct((DEVICES * SAMP, WIDTH), jnp.float32),
        in_specs=[
            pl.BlockSpec(memory_space=pltpu.SMEM),
            pl.BlockSpec(memory_space=pltpu.SMEM),
            pl.BlockSpec(memory_space=pltpu.VMEM),
        ],
        out_specs=pl.BlockSpec(memory_space=pltpu.VMEM),
        scratch_shapes=[pltpu.VMEM((IDS + 8, WIDTH), jnp.float32)] * blocks,
        compiler_params=pltpu.CompilerParams(vmem_limit_bytes=40 << 20),
        name="lookup",
    )(addr.reshape(-1), notes[:, 1, :SAMP].reshape(-1), held.reshape(TABLES * SPAN, WIDTH))
    parts = lax.all_to_all(
        partial.reshape(DEVICES, SAMP, WIDTH),
        "d",
        split_axis=0,
        concat_axis=0,
        tiled=True,
        axis_index_groups=EVERYONE,
    )
    return pl.pallas_call(
        finish_kernel,
        out_shape=jax.ShapeDtypeStruct((SAMP, TABLES, WIDTH), jnp.float32),
        in_specs=[
            pl.BlockSpec(memory_space=pltpu.SMEM),
            pl.BlockSpec(memory_space=pltpu.VMEM),
        ],
        out_specs=pl.BlockSpec(memory_space=pltpu.VMEM),
        name="finish",
    )(table_order, parts.reshape(4, TABLES, SAMP, WIDTH))


def solution(mesh):
    flat = Mesh(mesh.devices.reshape(DEVICES), ("d",))
    return jax.shard_map(
        body,
        mesh=flat,
        in_specs=(
            P(None, None, "d", None),
            P(),
            P(None, "d", None, None),
            P(None, "d", None),
            P(None, "d", None),
        ),
        out_specs=P("d", None, None),
        check_vma=False,
    )
```

time: 345 us -> 222 us (0.64)
  local copies, waits for them, and re-layouts: 107 us -> 1.03 us
  blocking collectives: 0 us -> 71.7 us
  waiting for transfers between devices: 166 us -> 109 us
  matrix products: 29 us -> 0 us
  Pallas kernels: 0 us -> 21.9 us
  starting transfers between devices: 28.8 us -> 8.63 us
    all_to_all x3 -> x1, waiting for transfers between devices: 166 us -> 109 us  [body(): lax.all_to_all(parcel, 'd', split_axis=0, concat_axis=0, tiled=True, axis...]
    gather x6 -> x0, local copies, waits for them, and re-layouts: 55.3 us -> none  [the longest x2 52.8 us: fetch_rows(): jnp.take(restored.reshape(per_group * row_count, columns), flat_index, ax...]
    all_to_all x0 -> x1, blocking collectives: none -> 45.7 us  [body(): lax.all_to_all(partial.reshape(DEVICES, SAMP, WIDTH), 'd', split_axis=0,...]
    dot_general x3 -> x0, matrix products: 29 us -> none  [the longest x1 15.6 us: body(): jnp.einsum('cu,uqd->cqd', picker, saved_rows.reshape(table_count, saved_d...]
    all_gather x0 -> x1, blocking collectives: none -> 25.9 us  [body(): lax.all_gather(notes, 'd', axis_index_groups=HOLDERS, axis=0, tiled=True)]
    pallas_call x0 -> x2, Pallas kernels: none -> 21.9 us  [the longest x1 19.7 us: body(): pl.pallas_call(lookup_kernel, out_shape=jax.ShapeDtypeStruct((DEVICES * S...]
    all_to_all x3 -> x1, starting transfers between devices: 28.8 us -> 8.63 us  [body(): lax.all_to_all(parcel, 'd', split_axis=0, concat_axis=0, tiled=True, axis...]
    unnamed x8 -> x1, local copies, waits for them, and re-layouts: 15.7 us -> 0.03 us
  transfers between devices with their start and end apart: 3 -> 1, of which waited for: 2 -> 1; matrix products, arithmetic and copies ran while one was open for 11% -> 0% of each run, Pallas kernels for 0% -> 0%
where the time goes in v1:
time: 222 us
  waiting for transfers between devices  109 us (49%)
  blocking collectives  71.7 us (32%)
  Pallas kernels  21.9 us (10%)
  other arithmetic  9.46 us (4%)
  starting transfers between devices  8.63 us (4%)
    all_to_all x1, waiting for transfers between devices, body(): lax.all_to_all(parcel, 'd', split_axis=0, concat_axis=0, tiled=True, axis...  109 us
    all_to_all x1, blocking collectives, body(): lax.all_to_all(partial.reshape(DEVICES, SAMP, WIDTH), 'd', split_axis=0,...  45.7 us
    all_gather x1, blocking collectives, body(): lax.all_gather(notes, 'd', axis_index_groups=HOLDERS, axis=0, tiled=True)  25.9 us
    pallas_call x1, Pallas kernels, body(): pl.pallas_call(lookup_kernel, out_shape=jax.ShapeDtypeStruct((DEVICES * S...  19.7 us
    all_to_all x1, starting transfers between devices, body(): lax.all_to_all(parcel, 'd', split_axis=0, concat_axis=0, tiled=True, axis...  8.63 us
    concatenate x1, other arithmetic, body(): jnp.concatenate([saved_rows.reshape(TABLES, DEPTH, WIDTH), jnp.pad(notes,...  7.31 us
  transfers between devices with their start and end apart: 1, of which 1 were waited for; matrix products, arithmetic and copies ran while one was open for 0% of the time, Pallas kernels for 0%

profile of v1, /device:TPU:1, one launch (start us, length us, event | category | flops | bytes accessed | tf_op | source)
XLA Modules:
  0.0 221.9 jit_solution(4533892368087774280)
XLA Ops:
  0.0 1.3 convert_reduce_fusion
  1.3 0.7 bitcast_add_fusion
  2.1 7.3 %select_maximum_fusion = f32[32,520,128]{2,1,0:T(8,128)} fusion(f32[32,2,128]{2,1,0:T(2,128)S(1)} %copy.16, f32[32,512,128]{2,1,0:T(8,128)} %bitcast.15), kind=kLoop, calls=%fused_computation | loop fusion | flops 6389760 | bytes 16941056 | tf_op jit(solution)/shard_map/concatenate | solution.py:70
  9.4 8.6 %all-to-all-start = ((f32[32,520,128]{2,1,0:T(8,128)}), f32[32,520,128]{2,1,0:T(8,128)}, u32[]{:S(2)}, u32[]{:S(2)}) async-start(f32[32,520,128]{2,1,0:T(8,128)} %select_maximum_fusion), calls=%async_computation | async-start | bytes 17039360 | tf_op jit(solution)/shard_map/all_to_all | solution.py:77
  18.1 109.2 %all-to-all-done = f32[32,520,128]{2,1,0:T(8,128)} async-done(((f32[32,520,128]{2,1,0:T(8,128)}), f32[32,520,128]{2,1,0:T(8,128)}, u32[]{:S(2)}, u32[]{:S(2)}) %all-to-all-start) | async-done | bytes 8519712 | tf_op jit(solution)/shard_map/all_to_all | solution.py:77
  127.3 0.9 slice.12
  128.2 25.9 %all_gather.3 = f32[128,2,128]{2,1,0:T(2,128)S(1)} all-gather(f32[32,2,128]{2,1,0:T(2,128)S(1)} %slice.12), channel_id=1, replica_groups={{0,22,104,126},{1,23,105,127},{16,38,120,78},{17,39,121,79},{32,54,72,9..., dimensions={0}, use_global_device_ids=true | all-gather | bytes 163840 | tf_op jit(solution)/shard_map/all_gather | solution.py:79
  154.2 0.1 reshape_squeeze.3.ends
  154.3 0.1 select_bitcast_fusion.addr
  154.3 19.7 %lookup.1 = f32[2048,128]{1,0:T(8,128)S(1)} custom-call(s32[16384]{0:T(1024)S(1)} %select_bitcast_fusion.addr, s32[2048]{0:T(1024)S(1)} %reshape_squeeze.3.ends, f32[16640,128]{1,0:T(8,128)} %bitcast.7.table), custom_call_target="tpu_custom_call" | custom-call | tf_op jit(solution)/shard_map/lookup/pallas_call | solution.py:86
  174.0 45.7 %all_to_all.10 = f32[128,16,128]{2,1,0:T(8,128)} all-to-all(f32[128,16,128]{2,1,0:T(8,128)S(1)} %bitcast.14), channel_id=1, replica_groups={{0,1,16,17,32,33,48,49,2,3,18,19,34,35,50,51,64,65,80,81,96,97,112,113,..., dimensions={0} | all-to-all | bytes 2097152 | tf_op jit(solution)/shard_map/all_to_all | solution.py:99
  219.7 2.2 finish.1
  (4 shorter events, 0.1 us)
Async XLA Ops:
  9.4 117.9 %all-to-all-start = ((f32[32,520,128]{2,1,0:T(8,128)}), f32[32,520,128]{2,1,0:T(8,128)}, u32[]{:S(2)}, u32[]{:S(2)}) async-start(f32[32,520,128]{2,1,0:T(8,128)} %select_maximum_fusion), calls=%async_computation | async-start | bytes 17039360 | tf_op jit(solution)/shard_map/all_to_all | solution.py:77

commit v2 on v1

v2 whole, which is shorter than its diff:
```python
import jax
import jax.numpy as jnp
from jax import lax
from jax.experimental import pallas as pl
from jax.experimental.pallas import tpu as pltpu
from jax.sharding import Mesh, PartitionSpec as P

TABLES = 32
DEPTH = 512
WIDTH = 128
DEVICES = 128
IDS = 128
SAMP = 16
SIZES = (32, 48, 64, 96, 128)
BLOCKS = 4


def place(k):
    return (k >> 6) * 2 + ((k >> 1) & 1), (k >> 4) & 3, (k >> 2) & 3, k & 1


def device(x, y, z, c):
    return (x >> 1) * 64 + y * 16 + z * 4 + (x & 1) * 2 + c


def label(k):
    x, y, z, c = place(k)
    return x * 8 + y * 2 + c


PLANES = [sorted((k for k in range(DEVICES) if place(k)[2] == z), key=label) for z in range(4)]


def moved(axis, by):
    pairs = []
    for k in range(DEVICES):
        at = list(place(k))
        at[axis] = (at[axis] + by) % (2 if axis == 3 else 4)
        pairs.append((k, device(*at)))
    return pairs


def spread(parts, mine, axis, along):
    size = 2 if axis == 3 else 4
    got = []
    for by in range(size):
        piece = lax.dynamic_index_in_dim(parts, (mine + by) & (size - 1), along, keepdims=False)
        got.append(piece if by == 0 else lax.ppermute(piece, "d", moved(axis, by)))
    return jnp.stack(got)


def lookup_kernel(me, addr, ends, table, out, *sums):
    x, y, z, c = place(me[0])

    def step(i, carry):
        first, count = [], []
        for j in range(BLOCKS):
            note = (i * BLOCKS + j) * IDS
            begin = ends[note + z * SAMP]
            first.append(note + begin)
            count.append(ends[note + z * SAMP + SAMP] - begin)
        most = count[0]
        for n in count[1:]:
            most = jnp.maximum(most, n)

        def gather(size):
            for j, prefix in enumerate(sums):
                total = jnp.zeros((1, WIDTH), jnp.float32)
                for p in range(size):
                    total = total + table[pl.ds(addr[first[j] + p], 1), :]
                    prefix[p + 1 : p + 2, :] = total

        below = -1
        for size in SIZES:
            pl.when((most > below) & (most <= size))(lambda size=size: gather(size))
            below = size

        for j, prefix in enumerate(sums):
            b = i * BLOCKS + j
            note = b * IDS + z * SAMP
            begin = ends[note]
            bx = (x - (b & 3)) & 3
            by = (y - ((b >> 2) & 3)) & 3
            bc = c ^ ((b >> 4) & 1)
            bz = (z - ((b >> 5) & 3)) & 3
            row = device(bx, by, bz, bc) * SAMP
            low = jnp.zeros((1, WIDTH), jnp.float32)
            for s in range(SAMP):
                upto = prefix[pl.ds(ends[note + s + 1] - begin, 1), :]
                out[pl.ds(row + s, 1), :] = upto - low
                low = upto
        return carry

    for prefix in sums:
        prefix[0:1, :] = jnp.zeros((1, WIDTH), jnp.float32)
    lax.fori_loop(0, DEVICES // BLOCKS, step, 0)


def finish_kernel(order, parts, out):
    for col in range(TABLES):
        t = order[col]
        x, y, c = t >> 3, (t >> 1) & 3, t & 1
        total = (parts[device(x, y, 0, c)] + parts[device(x, y, 1, c)]) + (
            parts[device(x, y, 2, c)] + parts[device(x, y, 3, c)]
        )
        out[:, col, :] = total


def body(saved_rows, table_order, owner_shard, row_in_shard, bag_owner):
    me = lax.axis_index("d")
    x, y, z, c = place(me)
    held = lax.all_to_all(
        saved_rows.reshape(TABLES, DEPTH, WIDTH),
        "d",
        split_axis=0,
        concat_axis=0,
        tiled=True,
        axis_index_groups=PLANES,
    )

    wanted = owner_shard[:, 0, :, 0] * 1024 + row_in_shard[:, 0, :]
    bags = bag_owner[:, 0, :]
    source = wanted & 127
    sx, sy, plane, sc = place(source)
    addr = (sx * 8 + sy * 2 + sc) * DEPTH + (wanted >> 7)
    lanes = jnp.arange(IDS, dtype=jnp.int32)
    is_in = (plane[:, None, :] == jnp.arange(4, dtype=jnp.int32)[None, :, None]).astype(jnp.float32)
    upto = (lanes[:, None] <= lanes[None, :]).astype(jnp.float32)
    rank = jnp.einsum("tzp,pq->tzq", is_in, upto)
    amount = rank[:, :, IDS - 1]
    offset = jnp.cumsum(amount, axis=1) - amount
    slot = jnp.sum(is_in * (rank + offset[:, :, None] - 1.0), axis=1).astype(jnp.int32)
    order = jnp.sum(
        jnp.where(slot[:, None, :] == lanes[None, :, None], addr[:, None, :], 0), axis=2
    )
    below = (bags[:, None, :] <= jnp.arange(SAMP, dtype=jnp.int32)[None, :, None]).astype(jnp.float32)
    ends = jnp.einsum("tzp,tbp->tzb", is_in, below) + offset[:, :, None]
    ends = jnp.pad(ends.reshape(TABLES, 4 * SAMP), ((0, 0), (1, IDS - 1 - 4 * SAMP)))
    notes = jnp.stack([order.astype(jnp.float32), ends], axis=1)

    notes = spread(notes.reshape(4, 4, 2, 2, IDS), x, 0, 0)
    notes = spread(notes, y, 1, 1)
    notes = spread(notes, c, 3, 2)
    notes = jnp.stack([notes] + [lax.ppermute(notes, "d", moved(2, by)) for by in (1, 2, 3)])
    notes = notes.reshape(DEVICES, 2, IDS).astype(jnp.int32)
    addr = jnp.pad(notes[:, 0].reshape(-1), (0, IDS))
    ends = notes[:, 1].reshape(-1)

    partial = pl.pallas_call(
        lookup_kernel,
        out_shape=jax.ShapeDtypeStruct((DEVICES * SAMP, WIDTH), jnp.float32),
        in_specs=[
            pl.BlockSpec(memory_space=pltpu.SMEM),
            pl.BlockSpec(memory_space=pltpu.SMEM),
            pl.BlockSpec(memory_space=pltpu.SMEM),
            pl.BlockSpec(memory_space=pltpu.VMEM),
        ],
        out_specs=pl.BlockSpec(memory_space=pltpu.VMEM),
        scratch_shapes=[pltpu.VMEM((IDS + 8, WIDTH), jnp.float32)] * BLOCKS,
        compiler_params=pltpu.CompilerParams(vmem_limit_bytes=40 << 20),
        name="lookup",
    )(me.reshape(1), addr, ends, held.reshape(TABLES * DEPTH, WIDTH))
    parts = lax.all_to_all(
        partial.reshape(DEVICES, SAMP, WIDTH), "d", split_axis=0, concat_axis=0, tiled=True
    )
    return pl.pallas_call(
        finish_kernel,
        out_shape=jax.ShapeDtypeStruct((SAMP, TABLES, WIDTH), jnp.float32),
        in_specs=[
            pl.BlockSpec(memory_space=pltpu.SMEM),
            pl.BlockSpec(memory_space=pltpu.VMEM),
        ],
        out_specs=pl.BlockSpec(memory_space=pltpu.VMEM),
        name="finish",
    )(table_order, parts)


def solution(mesh):
    flat = Mesh(mesh.devices.reshape(DEVICES), ("d",))
    return jax.shard_map(
        body,
        mesh=flat,
        in_specs=(
            P(None, None, "d", None),
            P(),
            P(None, "d", None, None),
            P(None, "d", None),
            P(None, "d", None),
        ),
        out_specs=P("d", None, None),
        check_vma=False,
    )
```

time: 222 us -> 191 us (0.86)
  blocking collectives: 71.7 us -> 24.9 us
  starting transfers between devices: 8.63 us -> 42.9 us
  other arithmetic: 9.46 us -> 1.36 us
  Pallas kernels: 21.9 us -> 16 us
  waiting for transfers between devices: 109 us -> 104 us
    all_to_all x1, waiting for transfers between devices: 109 us -> 0.01 us  [body(): lax.all_to_all(saved_rows.reshape(TABLES, DEPTH, WIDTH), 'd', split_axis=...]
    ppermute x0 -> x10, waiting for transfers between devices: none -> 104 us  [the longest x7 103 us: spread(): got.append(piece if by == 0 else lax.ppermute(piece, 'd', moved(axis, by)))]
    ppermute x0 -> x10, starting transfers between devices: none -> 34.1 us  [the longest x7 27.8 us: spread(): got.append(piece if by == 0 else lax.ppermute(piece, 'd', moved(axis, by)))]
    all_gather x1 -> x0, blocking collectives: 25.9 us -> none  [body(): lax.all_gather(notes, 'd', axis_index_groups=HOLDERS, axis=0, tiled=True)]
    all_to_all x1, blocking collectives: 45.7 us -> 24.9 us  [body(): lax.all_to_all(partial.reshape(DEVICES, SAMP, WIDTH), 'd', split_axis=0,...]
    concatenate x1 -> x0, other arithmetic: 7.31 us -> none  [body(): jnp.concatenate([saved_rows.reshape(TABLES, DEPTH, WIDTH), jnp.pad(notes,...]
    pallas_call x1, Pallas kernels: 19.7 us -> 13.8 us  [body(): pl.pallas_call(lookup_kernel, out_shape=jax.ShapeDtypeStruct((DEVICES * S...]
  transfers between devices with their start and end apart: 1 -> 11, of which waited for: 1 -> 5; matrix products, arithmetic and copies ran while one was open for 0% -> 1% of each run, Pallas kernels for 0% -> 0%
where the time goes in v2:
time: 191 us; the launch traced here: 190 us
  waiting for transfers between devices  104 us (54%)
  starting transfers between devices  42.9 us (22%)
  blocking collectives  24.9 us (13%)
  Pallas kernels  16 us (8%)
    ppermute x7, waiting for transfers between devices, spread(): got.append(piece if by == 0 else lax.ppermute(piece, 'd', moved(axis, by)))  103 us
    ppermute x7, starting transfers between devices, spread(): got.append(piece if by == 0 else lax.ppermute(piece, 'd', moved(axis, by)))  27.8 us
    all_to_all x1, blocking collectives, body(): lax.all_to_all(partial.reshape(DEVICES, SAMP, WIDTH), 'd', split_axis=0,...  24.9 us
    pallas_call x1, Pallas kernels, body(): pl.pallas_call(lookup_kernel, out_shape=jax.ShapeDtypeStruct((DEVICES * S...  13.8 us
    all_to_all x1, starting transfers between devices, body(): lax.all_to_all(saved_rows.reshape(TABLES, DEPTH, WIDTH), 'd', split_axis=...  8.78 us
    ppermute x3, starting transfers between devices, body(): lax.ppermute(notes, 'd', moved(2, by))  6.35 us
  transfers between devices with their start and end apart: 11, of which 5 were waited for; matrix products, arithmetic and copies ran while one was open for 1% of the time, Pallas kernels for 0%

profile of v2, /device:TPU:1, one launch (start us, length us, event | category | flops | bytes accessed | tf_op | source)
XLA Modules:
  0.0 190.2 jit_solution(1159951674114148563)
XLA Ops:
  0.0 8.8 %all-to-all-start = ((f32[32,512,128]{2,1,0:T(8,128)}), f32[32,512,128]{2,1,0:T(8,128)}, u32[]{:S(2)}, u32[]{:S(2)}) async-start(f32[32,512,128]{2,1,0:T(8,128)} %bitcast.55), calls=%async_computation | async-start | bytes 16777216 | tf_op jit(solution)/shard_map/all_to_all | solution.py:112
  8.9 0.1 fusion.3
  9.1 0.2 fusion.16
  9.4 0.1 select_reduce_fusion.1
  9.5 0.9 select_reduce_fusion
  10.4 0.2 convolution_add_fusion
  10.7 0.1 pad.8.clone
  10.8 1.4 collective-permute-start
  12.3 2.4 %collective-permute-start.1 = (f32[4,2,2,128]{3,1,0,2:T(2,128)S(1)}, f32[4,2,2,128]{3,1,0,2:T(2,128)S(1)}, u32[]{:S(2)}, u32[]{:S(2)}) collective-permute-start(f32[4,2,2,128]{3,1,0,2:T(2,128)S(1)} %get-tuple-element.17), channel_id=1, source_target_pairs={{0,64},{1,65},{2,66},{3,67},{4,68},{5,69},{6,70},{7,71},{8,72},{9,... | collective-permute-start | bytes 24584 | tf_op jit(solution)/shard_map/ppermute | solution.py:48
  14.7 1.1 collective-permute-start.2
  15.8 100.2 %collective-permute-done = f32[4,2,2,128]{3,1,0,2:T(2,128)S(1)} collective-permute-done((f32[4,2,2,128]{3,1,0,2:T(2,128)S(1)}, f32[4,2,2,128]{3,1,0,2:T(2,128)S(1)}, u32[]{:S(2)}, u32[]{:S(2)}) %collective-permute-start) | collective-permute-done | bytes 8224 | tf_op jit(solution)/shard_map/ppermute | solution.py:48
  116.1 0.2 collective-permute-done.1
  116.3 17.9 %collective-permute-start.3 = (f32[4,2,2,128]{3,2,1,0:T(2,128)S(1)}, f32[4,2,2,128]{3,2,1,0:T(2,128)S(1)}, u32[]{:S(2)}, u32[]{:S(2)}) collective-permute-start(f32[4,2,2,128]{3,2,1,0:T(2,128)S(1)} %bitcast.73), channel_id=1, source_target_pairs={{0,16},{1,17},{2,18},{3,19},{4,20},{5,21},{6,22},{7,23},{8,24},{9,... | collective-permute-start | bytes 24584 | tf_op jit(solution)/shard_map/ppermute | solution.py:48
  134.2 2.5 %collective-permute-start.5 = (f32[4,2,2,128]{3,2,1,0:T(2,128)S(1)}, f32[4,2,2,128]{3,2,1,0:T(2,128)S(1)}, u32[]{:S(2)}, u32[]{:S(2)}) collective-permute-start(f32[4,2,2,128]{3,2,1,0:T(2,128)S(1)} %bitcast.71), channel_id=1, source_target_pairs={{0,48},{1,49},{2,50},{3,51},{4,52},{5,53},{6,54},{7,55},{8,56},{9,... | collective-permute-start | bytes 24584 | tf_op jit(solution)/shard_map/ppermute | solution.py:48
  136.7 1.5 collective-permute-done.4
  138.3 2.4 %collective-permute-start.6 = (f32[4,4,2,128]{3,1,2,0:T(4,128)S(1)}, f32[4,4,2,128]{3,1,2,0:T(4,128)S(1)}, u32[]{:S(2)}, u32[]{:S(2)}) collective-permute-start(f32[4,4,2,128]{3,1,2,0:T(4,128)S(1)} %copy.57), channel_id=1, source_target_pairs={{0,1},{1,0},{2,3},{3,2},{4,5},{5,4},{6,7},{7,6},{8,9},{9,8},{10,11... | collective-permute-start | bytes 49160 | tf_op jit(solution)/shard_map/ppermute | solution.py:48
  140.7 0.8 collective-permute-done.6
  141.5 3.7 %collective-permute-start.8 = (f32[2,4,4,2,128]{4,2,3,1,0:T(4,128)S(1)}, f32[2,4,4,2,128]{4,2,3,1,0:T(4,128)S(1)}, u32[]{:S(2)}, u32[]{:S(2)}) collective-permute-start(f32[2,4,4,2,128]{4,2,3,1,0:T(4,128)S(1)} %get-tuple-element.8), channel_id=1, source_target_pairs={{0,8},{1,9},{2,10},{3,11},{4,12},{5,13},{6,14},{7,15},{8,0},{9,1},... | collective-permute-start | bytes 98312 | tf_op jit(solution)/shard_map/ppermute | solution.py:144
  145.2 0.7 collective-permute-start.7
  146.0 1.9 %collective-permute-start.9 = (f32[2,4,4,2,128]{4,2,3,1,0:T(4,128)S(1)}, f32[2,4,4,2,128]{4,2,3,1,0:T(4,128)S(1)}, u32[]{:S(2)}, u32[]{:S(2)}) collective-permute-start(f32[2,4,4,2,128]{4,2,3,1,0:T(4,128)S(1)} %get-tuple-element.8), channel_id=1, source_target_pairs={{0,12},{1,13},{2,14},{3,15},{4,0},{5,1},{6,2},{7,3},{8,4},{9,5},{1... | collective-permute-start | bytes 98312 | tf_op jit(solution)/shard_map/ppermute | solution.py:144
  147.9 1.3 collective-permute-done.7
  149.3 13.8 %lookup.1 = f32[2048,128]{1,0:T(8,128)S(1)} custom-call(s32[1]{0:T(128)} %bitcast.me, s32[16512]{0:T(1024)S(1)} %pad.9.addr, s32[16384]{0:T(1024)S(1)} %get-tuple-element.5.ends, f32[16384,128]{1,0:T(8,128)} %bitcast.34.table), custom_call_target="tpu_custom_call" | custom-call | tf_op jit(solution)/shard_map/lookup/pallas_call | solution.py:149
  163.1 24.9 %all_to_all.10.parts = f32[128,16,128]{2,1,0:T(8,128)} all-to-all(f32[128,16,128]{2,1,0:T(8,128)S(1)} %bitcast.54), channel_id=1, replica_groups=mesh['grp'=2,'row'=64] {'grp','row'}, dimensions={0} | all-to-all | bytes 2097152 | tf_op jit(solution)/shard_map/all_to_all | solution.py:163
  188.0 2.2 %finish.1 = f32[16,32,128]{2,1,0:T(8,128)} custom-call(s32[32]{0:T(128)} %order.1, f32[128,16,128]{2,1,0:T(8,128)} %all_to_all.10.parts), custom_call_target="tpu_custom_call" | custom-call | tf_op jit(solution)/shard_map/finish/pallas_call | solution.py:166
  (37 shorter events, 0.6 us)
Async XLA Ops:
  0.0 8.8 %copy-start = (s32[32,1,128,1]{2,3,1,0:T(1,128)S(1)}, s32[32,1,128,1]{2,3,1,0:T(1,128)}, u32[]{:S(2)}) copy-start(s32[32,1,128,1]{2,3,1,0:T(1,128)} %param.7) | copy-start | bytes 49156
  0.0 8.8 %copy-start.1 = (s32[32,1,128]{2,1,0:T(1,128)S(1)}, s32[32,1,128]{2,1,0:T(1,128)}, u32[]{:S(2)}) copy-start(s32[32,1,128]{2,1,0:T(1,128)} %param.8) | copy-start | bytes 49156
  0.0 10.4 %copy-start.2 = (s32[32,1,128]{2,1,0:T(1,128)S(1)}, s32[32,1,128]{2,1,0:T(1,128)}, u32[]{:S(2)}) copy-start(s32[32,1,128]{2,1,0:T(1,128)} %param.9) | copy-start | bytes 49156
  0.0 149.3 %all-to-all-start = ((f32[32,512,128]{2,1,0:T(8,128)}), f32[32,512,128]{2,1,0:T(8,128)}, u32[]{:S(2)}, u32[]{:S(2)}) async-start(f32[32,512,128]{2,1,0:T(8,128)} %bitcast.55), calls=%async_computation | async-start | bytes 16777216 | tf_op jit(solution)/shard_map/all_to_all | solution.py:112
  10.8 105.2 %collective-permute-start = (f32[4,2,2,128]{3,1,0,2:T(2,128)S(1)}, f32[4,2,2,128]{3,1,0,2:T(2,128)S(1)}, u32[]{:S(2)}, u32[]{:S(2)}) collective-permute-start(f32[4,2,2,128]{3,1,0,2:T(2,128)S(1)} %get-tuple-element.16), channel_id=1, source_target_pairs={{0,2},{1,3},{2,64},{3,65},{4,6},{5,7},{6,68},{7,69},{8,10},{9,11},... | collective-permute-start | bytes 24584 | tf_op jit(solution)/shard_map/ppermute | solution.py:48
  12.3 104.0 %collective-permute-start.1 = (f32[4,2,2,128]{3,1,0,2:T(2,128)S(1)}, f32[4,2,2,128]{3,1,0,2:T(2,128)S(1)}, u32[]{:S(2)}, u32[]{:S(2)}) collective-permute-start(f32[4,2,2,128]{3,1,0,2:T(2,128)S(1)} %get-tuple-element.17), channel_id=1, source_target_pairs={{0,64},{1,65},{2,66},{3,67},{4,68},{5,69},{6,70},{7,71},{8,72},{9,... | collective-permute-start | bytes 24584 | tf_op jit(solution)/shard_map/ppermute | solution.py:48
  14.7 101.5 %collective-permute-start.2 = (f32[4,2,2,128]{3,1,0,2:T(2,128)S(1)}, f32[4,2,2,128]{3,1,0,2:T(2,128)S(1)}, u32[]{:S(2)}, u32[]{:S(2)}) collective-permute-start(f32[4,2,2,128]{3,1,0,2:T(2,128)S(1)} %get-tuple-element.18), channel_id=1, source_target_pairs={{0,66},{1,67},{2,0},{3,1},{4,70},{5,71},{6,4},{7,5},{8,74},{9,75},... | collective-permute-start | bytes 24584 | tf_op jit(solution)/shard_map/ppermute | solution.py:48
  116.3 20.4 %collective-permute-start.3 = (f32[4,2,2,128]{3,2,1,0:T(2,128)S(1)}, f32[4,2,2,128]{3,2,1,0:T(2,128)S(1)}, u32[]{:S(2)}, u32[]{:S(2)}) collective-permute-start(f32[4,2,2,128]{3,2,1,0:T(2,128)S(1)} %bitcast.73), channel_id=1, source_target_pairs={{0,16},{1,17},{2,18},{3,19},{4,20},{5,21},{6,22},{7,23},{8,24},{9,... | collective-permute-start | bytes 24584 | tf_op jit(solution)/shard_map/ppermute | solution.py:48
  134.2 4.0 %collective-permute-start.4 = (f32[4,2,2,128]{3,2,1,0:T(2,128)S(1)}, f32[4,2,2,128]{3,2,1,0:T(2,128)S(1)}, u32[]{:S(2)}, u32[]{:S(2)}) collective-permute-start(f32[4,2,2,128]{3,2,1,0:T(2,128)S(1)} %bitcast.72), channel_id=1, source_target_pairs={{0,32},{1,33},{2,34},{3,35},{4,36},{5,37},{6,38},{7,39},{8,40},{9,... | collective-permute-start | bytes 24584 | tf_op jit(solution)/shard_map/ppermute | solution.py:48
  134.2 4.0 %collective-permute-start.5 = (f32[4,2,2,128]{3,2,1,0:T(2,128)S(1)}, f32[4,2,2,128]{3,2,1,0:T(2,128)S(1)}, u32[]{:S(2)}, u32[]{:S(2)}) collective-permute-start(f32[4,2,2,128]{3,2,1,0:T(2,128)S(1)} %bitcast.71), channel_id=1, source_target_pairs={{0,48},{1,49},{2,50},{3,51},{4,52},{5,53},{6,54},{7,55},{8,56},{9,... | collective-permute-start | bytes 24584 | tf_op jit(solution)/shard_map/ppermute | solution.py:48
  138.3 3.2 %collective-permute-start.6 = (f32[4,4,2,128]{3,1,2,0:T(4,128)S(1)}, f32[4,4,2,128]{3,1,2,0:T(4,128)S(1)}, u32[]{:S(2)}, u32[]{:S(2)}) collective-permute-start(f32[4,4,2,128]{3,1,2,0:T(4,128)S(1)} %copy.57), channel_id=1, source_target_pairs={{0,1},{1,0},{2,3},{3,2},{4,5},{5,4},{6,7},{7,6},{8,9},{9,8},{10,11... | collective-permute-start | bytes 49160 | tf_op jit(solution)/shard_map/ppermute | solution.py:48
  141.5 6.4 %collective-permute-start.8 = (f32[2,4,4,2,128]{4,2,3,1,0:T(4,128)S(1)}, f32[2,4,4,2,128]{4,2,3,1,0:T(4,128)S(1)}, u32[]{:S(2)}, u32[]{:S(2)}) collective-permute-start(f32[2,4,4,2,128]{4,2,3,1,0:T(4,128)S(1)} %get-tuple-element.8), channel_id=1, source_target_pairs={{0,8},{1,9},{2,10},{3,11},{4,12},{5,13},{6,14},{7,15},{8,0},{9,1},... | collective-permute-start | bytes 98312 | tf_op jit(solution)/shard_map/ppermute | solution.py:144
  145.2 4.0 %collective-permute-start.7 = (f32[2,4,4,2,128]{4,2,3,1,0:T(4,128)S(1)}, f32[2,4,4,2,128]{4,2,3,1,0:T(4,128)S(1)}, u32[]{:S(2)}, u32[]{:S(2)}) collective-permute-start(f32[2,4,4,2,128]{4,2,3,1,0:T(4,128)S(1)} %get-tuple-element.8), channel_id=1, source_target_pairs={{0,4},{1,5},{2,6},{3,7},{4,8},{5,9},{6,10},{7,11},{8,12},{9,13},{1... | collective-permute-start | bytes 98312 | tf_op jit(solution)/shard_map/ppermute | solution.py:144
  146.0 3.2 %collective-permute-start.9 = (f32[2,4,4,2,128]{4,2,3,1,0:T(4,128)S(1)}, f32[2,4,4,2,128]{4,2,3,1,0:T(4,128)S(1)}, u32[]{:S(2)}, u32[]{:S(2)}) collective-permute-start(f32[2,4,4,2,128]{4,2,3,1,0:T(4,128)S(1)} %get-tuple-element.8), channel_id=1, source_target_pairs={{0,12},{1,13},{2,14},{3,15},{4,0},{5,1},{6,2},{7,3},{8,4},{9,5},{1... | collective-permute-start | bytes 98312 | tf_op jit(solution)/shard_map/ppermute | solution.py:144
